TPU v7x, 32 devices: a whole 2x2x4 slice. The times are simulated.
32 devices in a mesh: seq: 16 (over z, y, core), head: 2 (over x).
Axes of the slice: x: 2, y: 2, z: 4, core: 2. Of those that a mesh axis runs over, the one named last changes fastest.
Arguments:
- tokens: bfloat16 [1, 8192, 2048], P(None, 'seq'), may hold values from -6 to 6
- qkv_weight: bfloat16 [2048, 3, 2048], P(None, None, 'head'), may hold values from -1 to 1
- persistent: bfloat16 [2, 128, 2048], P(None, None, 'head'), may hold values from -60 to 60
- rate_weight: float32 [2048], replicated, may hold values from -0.25 to 0.25
- forget_rate: float32 [1, 8192], P(None, 'seq'), may hold values from 9.765625e-07 to 0.0009765625
- momentum_decay: float32 [1], replicated, may hold values from 0.5 to 0.95
- forget_share: float32 [1], replicated, may hold values from 0.05 to 0.5
- memory: float32 [2048, 2, 4096], P('seq', None, 'head'), may hold values from -0.125 to 0.125
- momentum: float32 [2048, 2, 4096], P('seq', None, 'head'), may hold values from -0.0625 to 0.0625
Outputs:
- attended: bfloat16 [1, 8192, 2048], P(None, 'seq', 'head')
- memory_out: float32 [2048, 2, 4096], P('seq', None, 'head')
- momentum_out: float32 [2048, 2, 4096], P('seq', None, 'head')
All inputs are finite; a program needn't handle non-finite values.
Results may differ from a plain program's by a relative error of at most 0.01.
Values may be sent and summed in bfloat16 or wider, within the bound.
A program may use at most 128 MiB of HBM per device.

v0:
```python
import jax
import jax.numpy as jnp
from jax import lax
from jax.sharding import PartitionSpec as P

HEAD_DIM = 128


def entering(value, axis, combine, identity):
    size, mine = (lax.axis_size(axis), lax.axis_index(axis))
    everything = lax.all_gather(value, axis)
    start = jnp.broadcast_to(jnp.asarray(identity, value.dtype), value.shape)

    def hop(k, before):
        at = size - 1 - k
        reached = at > mine
        new = combine(before, everything[at])
        return jnp.where(reached, new, before)

    return lax.fori_loop(0, size, hop, start)


def add_pair(earlier, later):
    return earlier + later


def key_mask(count, persist_count):
    rows_at = jnp.arange(count)[:, None]
    column = jnp.arange(persist_count + 2 * count)[None, :]
    local_pos = jnp.where(
        column < persist_count + count, column - persist_count, column - persist_count - count
    )
    return (column < persist_count) | (local_pos <= rows_at)


def attend_local(query, keys, values, recalled, persistent):
    count = query.shape[0]
    heads_here = query.shape[1] // HEAD_DIM
    persist_count = persistent.shape[1]
    persist_keys = persistent[0].reshape(persist_count, heads_here, HEAD_DIM)
    persist_values = persistent[1].reshape(persist_count, heads_here, HEAD_DIM)
    recall_heads = recalled.reshape(count, heads_here, HEAD_DIM)
    all_keys = jnp.concatenate(
        [persist_keys, recall_heads, keys.reshape(count, heads_here, HEAD_DIM)], axis=0
    )
    all_values = jnp.concatenate(
        [persist_values, recall_heads, values.reshape(count, heads_here, HEAD_DIM)], axis=0
    )
    scores = jnp.einsum(
        "thd,nhd->htn",
        query.reshape(count, heads_here, HEAD_DIM),
        all_keys,
        preferred_element_type=jnp.float32,
    ) * HEAD_DIM ** (-0.5)
    visible = key_mask(count, persist_count)
    scores = jnp.where(visible[None], scores, -1e30)
    largest = jnp.max(scores, axis=2, keepdims=True)
    expo = jnp.exp(scores - largest)
    probs = (expo / jnp.sum(expo, axis=2, keepdims=True)).astype(jnp.bfloat16)
    result = jnp.einsum("htn,nhd->thd", probs, all_values, preferred_element_type=jnp.float32)
    return result.astype(jnp.bfloat16).reshape(count, heads_here * HEAD_DIM)


def memory_forward(query_full, keys_full, first, second):
    stacked = jnp.concatenate([query_full, keys_full], axis=0)
    preact = jnp.dot(stacked, first, preferred_element_type=jnp.float32)
    hidden = jax.nn.silu(preact).astype(jnp.bfloat16)
    partial_out = lax.dot_general(
        hidden, second, (((1,), (1,)), ((), ())), preferred_element_type=jnp.float32
    )
    return (preact, hidden, partial_out)


def reduce_terms(keys_full, errors_full, wdz, whid):
    grad_first = lax.dot_general(
        keys_full, wdz, (((0,), (0,)), ((), ())), preferred_element_type=jnp.float32
    )
    grad_second = lax.dot_general(
        errors_full, whid, (((0,), (0,)), ((), ())), preferred_element_type=jnp.float32
    )
    return lax.psum_scatter(
        jnp.stack([grad_first, grad_second], axis=1).astype(jnp.bfloat16),
        "seq",
        scatter_dimension=0,
        tiled=True,
    ).astype(jnp.float32)


def on_device(
    tokens,
    qkv_weight,
    persistent,
    rate_weight,
    forget_rate,
    momentum_decay,
    forget_share,
    memory,
    momentum,
):
    seg_len = tokens.shape[1]
    width = tokens.shape[2]
    steps_len = lax.axis_size("seq") * seg_len
    lr_scale = 2.0 / (width * steps_len) ** 0.5
    totals = jnp.sum(forget_rate, axis=1)
    later = entering(totals, "seq", add_pair, jnp.zeros_like(totals))
    tail = totals[:, None] - jnp.cumsum(forget_rate, axis=1) + later[:, None]
    weights_low = lax.all_gather(memory.astype(jnp.bfloat16), "seq", axis=0, tiled=True)
    first = weights_low[:, 0, :]
    second = weights_low[:, 1, :]
    inputs = tokens[0]
    proj = jnp.einsum("td,dkf->tkf", inputs, qkv_weight, preferred_element_type=jnp.float32).astype(
        jnp.bfloat16
    )
    query = proj[:, 0]
    keys = proj[:, 1]
    values = proj[:, 2]
    query_full = lax.all_gather(query, "head", axis=1, tiled=True)
    keys_full = lax.all_gather(keys, "head", axis=1, tiled=True)
    preact, hidden, partial_out = memory_forward(query_full, keys_full, first, second)
    summed = lax.psum_scatter(
        partial_out.astype(jnp.bfloat16), "head", scatter_dimension=1, tiled=True
    ).astype(jnp.float32)
    recalled = summed[:seg_len].astype(jnp.bfloat16)
    errors_here = (summed[seg_len:] - values.astype(jnp.float32)).astype(jnp.bfloat16)
    errors_full = lax.all_gather(errors_here, "head", axis=1, tiled=True)
    rate = lr_scale * jax.nn.sigmoid(
        jnp.dot(inputs.astype(jnp.float32), rate_weight, precision=lax.Precision.HIGHEST)
    )
    weight = rate * jnp.exp(-tail[0])
    key_pre = preact[seg_len:]
    key_hidden = hidden[seg_len:]
    sigm = jax.nn.sigmoid(key_pre)
    back = jnp.dot(errors_full, second, preferred_element_type=jnp.float32)
    dpre = back * sigm * (1.0 + key_pre * (1.0 - sigm))
    wdz = (weight[:, None] * dpre).astype(jnp.bfloat16)
    whid = (weight[:, None] * key_hidden.astype(jnp.float32)).astype(jnp.bfloat16)
    attended = attend_local(query, keys, values, recalled, persistent)
    grad = reduce_terms(keys_full, errors_full, wdz, whid)
    results = [attended]
    momentum = momentum_decay[0] * momentum - grad
    memory = (1.0 - forget_share[0]) * memory + momentum
    return (jnp.stack(results, axis=0), memory, momentum)


def solution(mesh):
    placed = (
        P(None, "seq", None),
        P(None, None, "head"),
        P(None, None, "head"),
        P(),
        P(None, "seq"),
        P(),
        P(),
        P("seq", None, "head"),
        P("seq", None, "head"),
    )
    return jax.shard_map(
        on_device,
        mesh=mesh,
        in_specs=placed,
        out_specs=(P(None, "seq", "head"), P("seq", None, "head"), P("seq", None, "head")),
        check_vma=False,
    )
```

profile of v0, /device:TPU:0, one launch (start us, length us, event | category | flops | bytes accessed | tf_op | source)
XLA Modules:
  0.0 597.3 jit_solution(6255151362418320822)
XLA Ops:
  7.2 1.5 copy-done
  8.8 9.8 %convolution_convert_fusion = bf16[512,3,1024]{2,0,1:T(8,128)(2,1)S(1)} fusion(bf16[2048,3,1024]{2,0,1:T(8,128)(2,1)} %param.12, bf16[1,512,2048]{2,1,0:T(8,128)(2,1)S(1)} %copy-done), kind=kOutput, calls=%fused_computation.35 | convolution fusion | flops 6444023808 | bytes 17825792 | tf_op jit(solution)/shard_map/td,dkf->tkf/dot_general | solution.py:111
  18.5 1.6 copy-done.3
  20.2 2.6 fusion.45
  22.8 0.7 all-gather.11.cloned.1.call-update
  23.6 3.7 copy.51
  27.4 31.4 %all-gather.13.cloned.1.call-done = bf16[512,1,2048]{2,0,1:T(8,128)(2,1)} async-done(((bf16[512,1,1024]{2,0,1:T(8,128)(2,1)}), bf16[512,1,2048]{2,0,1:T(8,128)(2,1)}) %all-gather.13.cloned.1.call-update) | async-done | bytes 2097168 | tf_op jit(solution)/shard_map/all_gather | solution.py:118
  58.8 34.7 %all-gather.11.cloned.1.call-done = bf16[512,1,2048]{2,0,1:T(8,128)(2,1)} async-done(((bf16[512,1,1024]{2,0,1:T(8,128)(2,1)}), bf16[512,1,2048]{2,0,1:T(8,128)(2,1)}) %all-gather.11.cloned.1.call-update) | async-done | bytes 2097168 | tf_op jit(solution)/shard_map/all_gather | solution.py:117
  93.4 128.7 %all-gather.7.cloned.1.call-done = bf16[2048,2,2048]{2,0,1:T(8,128)(2,1)} async-done(((bf16[128,2,2048]{2,0,1:T(8,128)(2,1)}), bf16[2048,2,2048]{2,0,1:T(8,128)(2,1)}) %all-gather.7.cloned.1.call-update) | async-done | bytes 16777232 | tf_op jit(solution)/shard_map/all_gather | solution.py:107
  222.1 16.0 %multiply_convert_fusion = (bf16[1024,2048]{1,0:T(8,128)(2,1)}, f32[1024,2048]{1,0:T(8,128)}) fusion(bf16[2048,2,2048]{2,0,1:T(8,128)(2,1)} %all-gather.7.cloned.1.call-done, bf16[512,2048]{1,0:T(8,128)(2,1)} %bitcast.115, bf16[512,2048]{1,0:T(8,128)(2,1)} %bitcast.116), kind=kOutput, calls=%fused_computation.14 | convolution fusion | flops 8608808960 | bytes 25165824 | tf_op jit(solution)/shard_map/dot_general | solution.py:66
  238.1 12.0 %fusion.10 = bf16[1024,2048]{1,0:T(8,128)(2,1)} fusion(bf16[1024,2048]{1,0:T(8,128)(2,1)} %get-tuple-element.139, bf16[2048,2,2048]{2,0,1:T(8,128)(2,1)S(1)} %copy-done.11), kind=kOutput, calls=%fused_computation.22 | convolution fusion | flops 8592031744 | bytes 16777216 | tf_op jit(solution)/shard_map/dot_general | solution.py:68
  250.7 52.2 %reduce-scatter.3.cloned.1.call-done = bf16[1024,1024]{1,0:T(8,128)(2,1)} async-done(((bf16[1024,2048]{1,0:T(8,128)(2,1)}), bf16[1024,1024]{1,0:T(8,128)(2,1)}) %reduce-scatter.3.cloned.1.call-update) | async-done | bytes 2097168 | tf_op jit(solution)/shard_map/reduce_scatter | solution.py:120
  302.9 2.9 fusion.23
  307.1 1.3 dynamic-update-slice
  308.4 33.0 %all-reduce = f32[16]{0:T(128)S(1)} all-reduce(f32[16]{0:T(128)S(1)} %dynamic-update-slice), channel_id=1, replica_groups=mesh['seq'=16,'head'=2] {'seq'}, use_global_device_ids=true, to_apply=%add | all-reduce | flops 16 | bytes 128
  342.1 22.3 %while.15 = (s32[]{:T(128)}, f32[1]{0:T(128)}, s32[]{:T(128)}, f32[16,1]{0,1:T(1,128)S(1)}, s32[]{:T(128)}, /*index=5*/s32[]{:T(128)}, s32[]{:T(128)}, s32[]{:T(128)}) while((s32[]{:T(128)}, f32[1]{0:T(128)}, s32[]{:T(128)}, f32[16,1]{0,1:T(1,128)S(1)}, s32[]{:T(128)}, /*index=5*/s32[]{:T(128)}, s32[]{:T(128)}, s32[]{:T(128)}) %tuple.65), condition=%wide.region_7.8_spmd, body=%wide.region_6.7_spmd.sunk | while | flops 9 | bytes 177 | solution.py:20
  343.4 0.7 constant_dynamic-slice_fusion.2
  344.8 0.7 constant_dynamic-slice_fusion.2
  346.2 0.7 constant_dynamic-slice_fusion.2
  347.6 0.7 constant_dynamic-slice_fusion.2
  349.0 0.7 constant_dynamic-slice_fusion.2
  350.4 0.7 constant_dynamic-slice_fusion.2
  351.8 0.7 constant_dynamic-slice_fusion.2
  356.0 0.7 constant_dynamic-slice_fusion.2
  357.4 0.7 constant_dynamic-slice_fusion.2
  361.5 0.7 constant_dynamic-slice_fusion.2
  362.9 0.7 constant_dynamic-slice_fusion.2
  364.3 1.7 fusion.25
  366.7 10.2 %convert_bitcast_fusion = bf16[2048,1,2048]{2,0,1:T(8,128)(2,1)} fusion(bf16[512,2048]{1,0:T(8,128)(2,1)} %all-gather.9.cloned.1.call-done, bf16[1024,2048]{1,0:T(8,128)(2,1)} %get-tuple-element.139, f32[512]{0:T(512)S(1)} %fusion.38), kind=kOutput, calls=%fused_computation.12 | convolution fusion | flops 4302307328 | bytes 12584960 | tf_op jit(solution)/shard_map/dot_general | solution.py:78
  377.0 15.5 %convert_bitcast_fusion.1 = bf16[2048,1,2048]{2,0,1:T(8,128)(2,1)} fusion(bf16[512,1,2048]{2,0,1:T(8,128)(2,1)} %all-gather.13.cloned.1.call-done, f32[1024,2048]{1,0:T(8,128)} %get-tuple-element.140, bf16[512,2048]{1,0:T(8,128)(2,1)} %all-gather.9.cloned.1.call-done, bf16[2048,2,2048]{2,0,1:T(8,128)(2,1)} %all-gather.7.cloned.1.call-done, f32[512]{0:T(512)S(1)} %fusion.38), kind=kOutput, calls=%fused_computation.13 | convolution fusion | flops 8604614656 | bytes 25167872 | tf_op jit(solution)/shard_map/dot_general | solution.py:75
  392.4 13.8 %pad_maximum_fusion = bf16[2048,2,2048]{2,0,1:T(8,128)(2,1)} fusion(bf16[2048,1,2048]{2,0,1:T(8,128)(2,1)} %convert_bitcast_fusion, bf16[2048,1,2048]{2,0,1:T(8,128)(2,1)} %convert_bitcast_fusion.1), kind=kLoop, calls=%fused_computation.7 | loop fusion | flops 8388608 | bytes 33554432 | tf_op jit(solution)/shard_map/stack | solution.py:82
  408.4 0.7 fusion.46
  409.1 0.8 copy.38
  410.0 1.1 copy.28
  411.1 1.5 copy.37
  412.6 1.8 copy.23
  414.9 1.9 slice_bitcast_fusion.10
  416.8 1.2 copy.53
  418.0 1.2 copy.40
  419.3 2.5 copy.25
  421.7 10.9 %fusion.2 = f32[8,512,1152]{2,1,0:T(8,128)} fusion(pred[512,1152]{1,0:T(8,128)(4,1)S(1)} %fusion.21, bf16[512,8,128]{2,0,1:T(8,128)(2,1)S(1)} %copy.30, bf16[512,8,128]{2,0,1:T(8,128)(2,1)} %bitcast.103, bf16[128,8,128]{2,0,1:T(8,128)(2,1)S(1)} %copy.28, bf16[512,8,128]{2,1,0:T(8,128)(2,1)S(1)} %bitcast.102), kind=kOutput, calls=%fused_computation.4 | convolution fusion | flops 1224474624 | bytes 22872064 | tf_op jit(solution)/shard_map/thd,nhd->htn/dot_general | solution.py:49
  432.6 15.6 %exponential_reduce_fusion = f32[8,512]{1,0:T(8,128)S(1)} fusion(f32[8,512,1152]{2,1,0:T(8,128)} %fusion.2), kind=kOutput, calls=%fused_computation.6 | output fusion | flops 9438335 | bytes 18890752 | tf_op jit(solution)/shard_map/sub | solution.py:58
  448.3 21.1 %fusion.29 = bf16[8,128,512]{2,1,0:T(8,128)(2,1)} fusion(f32[8,512]{1,0:T(8,128)S(1)} %exponential_reduce_fusion, bf16[512,8,128]{0,2,1:T(8,128)(2,1)S(1)} %bitcast.106, bf16[512,8,128]{0,2,1:T(8,128)(2,1)} %copy.25, bf16[128,8,128]{0,2,1:T(8,128)(2,1)S(1)} %bitcast.109, f32[8,512,1152]{2,1,0:T(8,128)} %fusion.2), kind=kOutput, calls=%fused_computation.47 | convolution fusion | flops 1229722752 | bytes 22298624 | tf_op jit(solution)/shard_map/htn,nhd->thd/dot_general | solution.py:60
  469.4 2.5 copy.34
  471.9 108.0 %reduce-scatter.5.cloned.1.call-done = bf16[128,2,2048]{2,0,1:T(8,128)(2,1)} async-done(((bf16[2048,2,2048]{2,0,1:T(8,128)(2,1)}), bf16[128,2,2048]{2,0,1:T(8,128)(2,1)}) %reduce-scatter.5.cloned.1.call-update) | async-done | bytes 1048592 | tf_op jit(solution)/shard_map/reduce_scatter | solution.py:81
  579.9 4.4 multiply_add_fusion
  584.3 2.9 copy.35
  587.3 2.9 copy.36
  (56 shorter events, 7.9 us)
Async XLA Ops:
  7.2 1.6 copy-start
  7.2 51.6 %all-gather.13.cloned.1.call-start = ((), (), s32[]{:S(2)}) async-start(), calls=%async_computation.7 | async-start | bytes 3145728 | tf_op jit(solution)/shard_map/all_gather | solution.py:118
  18.5 1.6 copy-start.3
  22.8 70.6 %all-gather.11.cloned.1.call-start = ((), (), s32[]{:S(2)}) async-start(), calls=%async_computation.6 | async-start | bytes 3145728 | tf_op jit(solution)/shard_map/all_gather | solution.py:117
  23.5 198.6 %all-gather.7.cloned.1.call-start = ((), (), s32[]{:S(2)}) async-start(), calls=%async_computation.2 | async-start | bytes 17825792 | tf_op jit(solution)/shard_map/all_gather | solution.py:107
  27.3 275.5 %reduce-scatter.3.cloned.1.call-start = ((), (), s32[]{:S(2)}) async-start(), calls=%async_computation.3 | async-start | bytes 6291456 | tf_op jit(solution)/shard_map/reduce_scatter | solution.py:120
  222.1 16.0 %copy-start.11 = (bf16[2048,2,2048]{2,0,1:T(8,128)(2,1)S(1)}, bf16[2048,2,2048]{2,0,1:T(8,128)(2,1)}, u32[]{:S(2)}) copy-start(bf16[2048,2,2048]{2,0,1:T(8,128)(2,1)} %all-gather.7.cloned.1.call-done) | copy-start | bytes 50331652
  250.1 55.7 %copy-start.12 = (u32[32]{0:T(128)S(1)}, u32[32]{0:T(128)}, u32[]{:S(2)}) copy-start(u32[32]{0:T(128)} %constant.85) | copy-start | bytes 388
  250.1 56.4 %copy-start.10 = (f32[1,512]{1,0:T(1,128)S(1)}, f32[1,512]{1,0:T(1,128)}, u32[]{:S(2)}) copy-start(f32[1,512]{1,0:T(1,128)} %param.15) | copy-start | bytes 6148
  250.1 114.2 %copy-start.9 = (f32[2048]{0:T(1024)S(1)}, f32[2048]{0:T(1024)}, u32[]{:S(2)}) copy-start(f32[2048]{0:T(1024)} %param.14) | copy-start | bytes 24580
  250.1 116.6 %all-gather.9.cloned.1.call-start = ((), (), s32[]{:S(2)}) async-start(), calls=%async_computation.4 | async-start | bytes 3145728 | tf_op jit(solution)/shard_map/all_gather | solution.py:125
  305.8 274.2 %reduce-scatter.5.cloned.1.call-start = ((), (), s32[]{:S(2)}) async-start(), calls=%async_computation.5 | async-start | bytes 17825792 | tf_op jit(solution)/shard_map/reduce_scatter | solution.py:81
  406.2 1.9 copy-start.5
  406.3 2.1 copy-start.7
  407.7 3.5 copy-start.4
  432.6 15.6 %copy-start.6 = (bf16[512,1,1024]{0,2,1:T(8,128)(2,1)S(1)}, bf16[512,1,1024]{0,2,1:T(8,128)(2,1)}, u32[]{:S(2)}) copy-start(bf16[512,1,1024]{0,2,1:T(8,128)(2,1)} %copy.37) | copy-start | bytes 3145732
  432.6 15.6 %copy-start.8 = (bf16[1,128,1024]{1,2,0:T(8,128)(2,1)S(1)}, bf16[1,128,1024]{1,2,0:T(8,128)(2,1)}, u32[]{:S(2)}) copy-start(bf16[1,128,1024]{1,2,0:T(8,128)(2,1)} %copy.23) | copy-start | bytes 786436
  448.3 131.7 %copy-start.2 = (f32[128,2,2048]{2,1,0:T(2,128)S(1)}, f32[128,2,2048]{2,1,0:T(2,128)}, u32[]{:S(2)}) copy-start(f32[128,2,2048]{2,1,0:T(2,128)} %param.18) | copy-start | bytes 6291460
  584.3 5.9 copy-start.1
Sparse Core Ops, SparseCore 0:
  22.9 35.8 all-gather.12
  60.3 33.0 all-gather.10
  95.6 126.4 all-gather.6
  250.3 52.5 reduce-scatter.2
  305.9 33.0 all-gather.8
  406.4 173.5 reduce-scatter.4
where the time goes:
time: 606 us; the launch traced here: 597 us
  waiting for transfers between devices  356 us (59%)
  matrix products  97.2 us (16%)
  local copies, waits for them, and re-layouts  44.4 us (7%)
  other arithmetic  38.7 us (6%)
  blocking collectives  33 us (5%)
  between operations  16 us (3%)
  loops' own time  11.6 us (2%)
    all_gather x1, waiting for transfers between devices, on_device(): lax.all_gather(memory.astype(jnp.bfloat16), 'seq', axis=0, tiled=True)  129 us
    reduce_scatter x1, waiting for transfers between devices, reduce_terms(): lax.psum_scatter(jnp.stack([grad_first, grad_second], axis=1).astype(jnp....  108 us
    reduce_scatter x1, waiting for transfers between devices, on_device(): lax.psum_scatter(partial_out.astype(jnp.bfloat16), 'head', scatter_dimens...  52.2 us
    all_gather x1, waiting for transfers between devices, on_device(): query_full = lax.all_gather(query, 'head', axis=1, tiled=True)  34.7 us
    unnamed x1, blocking collectives  33 us
    all_gather x1, waiting for transfers between devices, on_device(): keys_full = lax.all_gather(keys, 'head', axis=1, tiled=True)  31.4 us
    unnamed x38, local copies, waits for them, and re-layouts  21.8 us
    dot_general x1, matrix products, attend_local(): jnp.einsum('htn,nhd->thd', probs, all_values, preferred_element_type=jnp....  21.1 us
  transfers between devices with their start and end apart: 6, of which 5 were waited for; matrix products, arithmetic and copies ran while one was open for 14% of the time, Pallas kernels for 0%

commit v1 on v0

--- a/solution.py
+++ b/solution.py
@@ -115,7 +115,8 @@
     keys = proj[:, 1]
     values = proj[:, 2]
     query_full = lax.all_gather(query, "head", axis=1, tiled=True)
-    keys_full = lax.all_gather(keys, "head", axis=1, tiled=True)
+    blocks = lax.all_gather(keys, "head")
+    keys_full = jnp.concatenate(blocks, axis=1)
     preact, hidden, partial_out = memory_forward(query_full, keys_full, first, second)
     summed = lax.psum_scatter(
         partial_out.astype(jnp.bfloat16), "head", scatter_dimension=1, tiled=True

time: 606 us -> 600 us (0.990)
    unnamed x38 -> x40, local copies, waits for them, and re-layouts: 21.8 us -> 22 us
  transfers between devices with their start and end apart: 6 -> 6, of which waited for: 5 -> 5; matrix products, arithmetic and copies ran while one was open for 14% -> 15% of each run, Pallas kernels for 0% -> 0%
where the time goes in v1:
time: 600 us; the launch traced here: 596 us
  waiting for transfers between devices  353 us (59%)
  matrix products  96.7 us (16%)
  local copies, waits for them, and re-layouts  46.7 us (8%)
  other arithmetic  38.8 us (6%)
  blocking collectives  33.5 us (6%)
  between operations  16 us (3%)
  loops' own time  10.7 us (2%)
    all_gather x1, waiting for transfers between devices, on_device(): lax.all_gather(memory.astype(jnp.bfloat16), 'seq', axis=0, tiled=True)  129 us
    reduce_scatter x1, waiting for transfers between devices, reduce_terms(): lax.psum_scatter(jnp.stack([grad_first, grad_second], axis=1).astype(jnp....  108 us
    reduce_scatter x1, waiting for transfers between devices, on_device(): lax.psum_scatter(partial_out.astype(jnp.bfloat16), 'head', scatter_dimens...  52.6 us
    unnamed x1, blocking collectives  33.5 us
    all_gather x1, waiting for transfers between devices, on_device(): query_full = lax.all_gather(query, 'head', axis=1, tiled=True)  31.5 us
    all_gather x1, waiting for transfers between devices, on_device(): blocks = lax.all_gather(keys, 'head')  31.1 us
    unnamed x40, local copies, waits for them, and re-layouts  22 us
    dot_general x1, matrix products, attend_local(): jnp.einsum('htn,nhd->thd', probs, all_values, preferred_element_type=jnp....  21.1 us
  transfers between devices with their start and end apart: 6, of which 5 were waited for; matrix products, arithmetic and copies ran while one was open for 15% of the time, Pallas kernels for 0%

profile of v1, /device:TPU:0, one launch (start us, length us, event | category | flops | bytes accessed | tf_op | source)
XLA Modules:
  0.0 595.8 jit_solution(4973615449533981255)
XLA Ops:
  7.2 1.5 copy-done
  8.8 9.8 %convolution_convert_fusion = bf16[512,3,1024]{2,0,1:T(8,128)(2,1)S(1)} fusion(bf16[2048,3,1024]{2,0,1:T(8,128)(2,1)} %param.12, bf16[1,512,2048]{2,1,0:T(8,128)(2,1)S(1)} %copy-done), kind=kOutput, calls=%fused_computation.35 | convolution fusion | flops 6444023808 | bytes 17825792 | tf_op jit(solution)/shard_map/td,dkf->tkf/dot_general | solution.py:111
  18.5 1.8 copy-done.3
  20.3 2.6 fusion.44
  23.0 0.7 all-gather.11.cloned.1.call-update
  23.7 3.7 copy.54
  27.8 31.1 %all-gather.13.cloned.1.call-done = bf16[1024,1,1024]{2,0,1:T(8,128)(2,1)} async-done(((bf16[512,1,1024]{2,0,1:T(8,128)(2,1)}), bf16[1024,1,1024]{2,0,1:T(8,128)(2,1)}) %all-gather.13.cloned.1.call-update) | async-done | bytes 2097168 | tf_op jit(solution)/shard_map/all_gather | solution.py:118
  58.9 3.2 copy.42
  62.0 31.5 %all-gather.11.cloned.1.call-done = bf16[512,1,2048]{2,0,1:T(8,128)(2,1)} async-done(((bf16[512,1,1024]{2,0,1:T(8,128)(2,1)}), bf16[512,1,2048]{2,0,1:T(8,128)(2,1)}) %all-gather.11.cloned.1.call-update) | async-done | bytes 2097168 | tf_op jit(solution)/shard_map/all_gather | solution.py:117
  93.6 128.7 %all-gather.7.cloned.1.call-done = bf16[2048,2,2048]{2,0,1:T(8,128)(2,1)} async-done(((bf16[128,2,2048]{2,0,1:T(8,128)(2,1)}), bf16[2048,2,2048]{2,0,1:T(8,128)(2,1)}) %all-gather.7.cloned.1.call-update) | async-done | bytes 16777232 | tf_op jit(solution)/shard_map/all_gather | solution.py:107
  222.2 16.0 %multiply_convert_fusion = (bf16[1024,2048]{1,0:T(8,128)(2,1)}, f32[1024,2048]{1,0:T(8,128)}) fusion(bf16[2048,2,2048]{2,0,1:T(8,128)(2,1)} %all-gather.7.cloned.1.call-done, bf16[512,2048]{1,0:T(8,128)(2,1)} %bitcast.109, bf16[512,2048]{1,0:T(8,128)(2,1)} %bitcast.121), kind=kOutput, calls=%fused_computation.14 | convolution fusion | flops 8608808960 | bytes 25165824 | tf_op jit(solution)/shard_map/dot_general | solution.py:66
  238.3 12.0 %fusion.10 = bf16[1024,2048]{1,0:T(8,128)(2,1)} fusion(bf16[1024,2048]{1,0:T(8,128)(2,1)} %get-tuple-element.139, bf16[2048,2,2048]{2,0,1:T(8,128)(2,1)S(1)} %copy-done.12), kind=kOutput, calls=%fused_computation.22 | convolution fusion | flops 8592031744 | bytes 16777216 | tf_op jit(solution)/shard_map/dot_general | solution.py:68
  250.4 52.6 %reduce-scatter.3.cloned.1.call-done = bf16[1024,1024]{1,0:T(8,128)(2,1)} async-done(((bf16[1024,2048]{1,0:T(8,128)(2,1)}), bf16[1024,1024]{1,0:T(8,128)(2,1)}) %reduce-scatter.3.cloned.1.call-update) | async-done | bytes 2097168 | tf_op jit(solution)/shard_map/reduce_scatter | solution.py:121
  303.0 2.9 fusion.23
  306.0 0.6 dynamic-slice
  306.7 0.6 reduce_sum.19
  307.3 1.4 dynamic-update-slice
  308.6 33.5 %all-reduce = f32[16]{0:T(128)S(1)} all-reduce(f32[16]{0:T(128)S(1)} %dynamic-update-slice), channel_id=1, replica_groups=mesh['seq'=16,'head'=2] {'seq'}, use_global_device_ids=true, to_apply=%add | all-reduce | flops 16 | bytes 128
  342.8 20.5 %while.15 = (s32[]{:T(128)}, f32[1]{0:T(128)}, s32[]{:T(128)}, f32[16,1]{0,1:T(1,128)S(1)}, s32[]{:T(128)}, /*index=5*/s32[]{:T(128)}, s32[]{:T(128)}, s32[]{:T(128)}) while((s32[]{:T(128)}, f32[1]{0:T(128)}, s32[]{:T(128)}, f32[16,1]{0,1:T(1,128)S(1)}, s32[]{:T(128)}, /*index=5*/s32[]{:T(128)}, s32[]{:T(128)}, s32[]{:T(128)}) %tuple.65), condition=%wide.region_7.8_spmd, body=%wide.region_6.7_spmd.sunk | while | flops 9 | bytes 177 | solution.py:20
  344.1 0.6 constant_dynamic-slice_fusion.2
  345.4 0.6 constant_dynamic-slice_fusion.2
  346.7 0.6 constant_dynamic-slice_fusion.2
  347.9 0.6 constant_dynamic-slice_fusion.2
  349.2 0.6 constant_dynamic-slice_fusion.2
  350.5 0.6 constant_dynamic-slice_fusion.2
  351.8 0.6 constant_dynamic-slice_fusion.2
  363.3 1.7 fusion.25
  365.1 0.7 fusion.38
  365.8 10.2 %convert_bitcast_fusion = bf16[2048,1,2048]{2,0,1:T(8,128)(2,1)} fusion(bf16[512,2048]{1,0:T(8,128)(2,1)} %all-gather.9.cloned.1.call-done, bf16[1024,2048]{1,0:T(8,128)(2,1)} %get-tuple-element.139, f32[512]{0:T(512)S(1)} %fusion.38), kind=kOutput, calls=%fused_computation.12 | convolution fusion | flops 4302307328 | bytes 12584960 | tf_op jit(solution)/shard_map/dot_general | solution.py:78
  376.1 14.9 %convert_bitcast_fusion.1 = bf16[2048,1,2048]{2,0,1:T(8,128)(2,1)} fusion(bf16[512,2048]{1,0:T(8,128)(2,1)S(1)} %bitcast.110, f32[1024,2048]{1,0:T(8,128)} %get-tuple-element.140, bf16[512,2048]{1,0:T(8,128)(2,1)} %all-gather.9.cloned.1.call-done, bf16[2048,2,2048]{2,0,1:T(8,128)(2,1)} %all-gather.7.cloned.1.call-done, f32[512]{0:T(512)S(1)} %fusion.38), kind=kOutput, calls=%fused_computation.13 | convolution fusion | flops 8604614656 | bytes 25167872 | tf_op jit(solution)/shard_map/dot_general | solution.py:75
  391.0 13.8 %pad_maximum_fusion = bf16[2048,2,2048]{2,0,1:T(8,128)(2,1)} fusion(bf16[2048,1,2048]{2,0,1:T(8,128)(2,1)} %convert_bitcast_fusion, bf16[2048,1,2048]{2,0,1:T(8,128)(2,1)} %convert_bitcast_fusion.1), kind=kLoop, calls=%fused_computation.7 | loop fusion | flops 8388608 | bytes 33554432 | tf_op jit(solution)/shard_map/stack | solution.py:82
  406.9 0.7 fusion.45
  407.7 0.8 copy.40
  408.5 1.1 copy.30
  409.7 1.5 copy.39
  411.2 1.8 copy.24
  413.4 1.9 slice_bitcast_fusion.10
  415.4 1.2 copy.56
  416.5 1.2 copy.43
  417.8 2.5 copy.27
  420.3 10.9 %fusion.2 = f32[8,512,1152]{2,1,0:T(8,128)} fusion(pred[512,1152]{1,0:T(8,128)(4,1)S(1)} %fusion.21, bf16[512,8,128]{2,0,1:T(8,128)(2,1)S(1)} %copy.32, bf16[512,8,128]{2,0,1:T(8,128)(2,1)} %bitcast.106, bf16[128,8,128]{2,0,1:T(8,128)(2,1)S(1)} %copy.30, bf16[512,8,128]{2,1,0:T(8,128)(2,1)S(1)} %bitcast.105), kind=kOutput, calls=%fused_computation.4 | convolution fusion | flops 1224474624 | bytes 22872064 | tf_op jit(solution)/shard_map/thd,nhd->htn/dot_general | solution.py:49
  431.2 15.6 %exponential_reduce_fusion = f32[8,512]{1,0:T(8,128)S(1)} fusion(f32[8,512,1152]{2,1,0:T(8,128)} %fusion.2), kind=kOutput, calls=%fused_computation.6 | output fusion | flops 9438335 | bytes 18890752 | tf_op jit(solution)/shard_map/sub | solution.py:58
  446.8 21.1 %fusion.29 = bf16[8,128,512]{2,1,0:T(8,128)(2,1)} fusion(f32[8,512]{1,0:T(8,128)S(1)} %exponential_reduce_fusion, bf16[512,8,128]{0,2,1:T(8,128)(2,1)S(1)} %bitcast.112, bf16[512,8,128]{0,2,1:T(8,128)(2,1)} %copy.27, bf16[128,8,128]{0,2,1:T(8,128)(2,1)S(1)} %bitcast.115, f32[8,512,1152]{2,1,0:T(8,128)} %fusion.2), kind=kOutput, calls=%fused_computation.47 | convolution fusion | flops 1229722752 | bytes 22298624 | tf_op jit(solution)/shard_map/htn,nhd->thd/dot_general | solution.py:60
  467.9 2.5 copy.36
  470.4 108.0 %reduce-scatter.5.cloned.1.call-done = bf16[128,2,2048]{2,0,1:T(8,128)(2,1)} async-done(((bf16[2048,2,2048]{2,0,1:T(8,128)(2,1)}), bf16[128,2,2048]{2,0,1:T(8,128)(2,1)}) %reduce-scatter.5.cloned.1.call-update) | async-done | bytes 1048592 | tf_op jit(solution)/shard_map/reduce_scatter | solution.py:81
  578.5 4.4 multiply_add_fusion
  582.8 2.9 copy.37
  585.8 2.9 copy.38
  (59 shorter events, 8.1 us)
Async XLA Ops:
  7.2 1.6 copy-start
  7.2 51.7 %all-gather.13.cloned.1.call-start = ((), (), s32[]{:S(2)}) async-start(), calls=%async_computation.7 | async-start | bytes 3145728 | tf_op jit(solution)/shard_map/all_gather | solution.py:118
  18.5 1.8 copy-start.3
  22.9 70.6 %all-gather.11.cloned.1.call-start = ((), (), s32[]{:S(2)}) async-start(), calls=%async_computation.6 | async-start | bytes 3145728 | tf_op jit(solution)/shard_map/all_gather | solution.py:117
  23.7 198.6 %all-gather.7.cloned.1.call-start = ((), (), s32[]{:S(2)}) async-start(), calls=%async_computation.2 | async-start | bytes 17825792 | tf_op jit(solution)/shard_map/all_gather | solution.py:107
  27.5 275.5 %reduce-scatter.3.cloned.1.call-start = ((), (), s32[]{:S(2)}) async-start(), calls=%async_computation.3 | async-start | bytes 6291456 | tf_op jit(solution)/shard_map/reduce_scatter | solution.py:121
  222.2 16.0 %copy-start.12 = (bf16[2048,2,2048]{2,0,1:T(8,128)(2,1)S(1)}, bf16[2048,2,2048]{2,0,1:T(8,128)(2,1)}, u32[]{:S(2)}) copy-start(bf16[2048,2,2048]{2,0,1:T(8,128)(2,1)} %all-gather.7.cloned.1.call-done) | copy-start | bytes 50331652
  250.3 55.7 %copy-start.13 = (u32[32]{0:T(128)S(1)}, u32[32]{0:T(128)}, u32[]{:S(2)}) copy-start(u32[32]{0:T(128)} %constant.85) | copy-start | bytes 388
  250.3 56.4 %copy-start.11 = (f32[1,512]{1,0:T(1,128)S(1)}, f32[1,512]{1,0:T(1,128)}, u32[]{:S(2)}) copy-start(f32[1,512]{1,0:T(1,128)} %param.15) | copy-start | bytes 6148
  250.3 113.0 %copy-start.10 = (f32[2048]{0:T(1024)S(1)}, f32[2048]{0:T(1024)}, u32[]{:S(2)}) copy-start(f32[2048]{0:T(1024)} %param.14) | copy-start | bytes 24580
  250.3 115.5 %all-gather.9.cloned.1.call-start = ((), (), s32[]{:S(2)}) async-start(), calls=%async_computation.4 | async-start | bytes 3145728 | tf_op jit(solution)/shard_map/all_gather | solution.py:126
  306.0 272.5 %reduce-scatter.5.cloned.1.call-start = ((), (), s32[]{:S(2)}) async-start(), calls=%async_computation.5 | async-start | bytes 17825792 | tf_op jit(solution)/shard_map/reduce_scatter | solution.py:81
  365.8 10.3 %copy-start.6 = (bf16[2,64,8,1024]{3,2,0,1:T(8,128)(2,1)S(1)}, bf16[2,64,8,1024]{3,2,0,1:T(8,128)(2,1)}, u32[]{:S(2)}) copy-start(bf16[2,64,8,1024]{3,2,0,1:T(8,128)(2,1)} %copy.42) | copy-start | bytes 6291460
  404.8 1.9 copy-start.5
  404.8 2.1 copy-start.8
  406.2 3.5 copy-start.4
  431.2 15.6 %copy-start.7 = (bf16[512,1,1024]{0,2,1:T(8,128)(2,1)S(1)}, bf16[512,1,1024]{0,2,1:T(8,128)(2,1)}, u32[]{:S(2)}) copy-start(bf16[512,1,1024]{0,2,1:T(8,128)(2,1)} %copy.39) | copy-start | bytes 3145732
  431.2 15.6 %copy-start.9 = (bf16[1,128,1024]{1,2,0:T(8,128)(2,1)S(1)}, bf16[1,128,1024]{1,2,0:T(8,128)(2,1)}, u32[]{:S(2)}) copy-start(bf16[1,128,1024]{1,2,0:T(8,128)(2,1)} %copy.24) | copy-start | bytes 786436
  446.8 131.7 %copy-start.2 = (f32[128,2,2048]{2,1,0:T(2,128)S(1)}, f32[128,2,2048]{2,1,0:T(2,128)}, u32[]{:S(2)}) copy-start(f32[128,2,2048]{2,1,0:T(2,128)} %param.18) | copy-start | bytes 6291460
  582.8 5.9 copy-start.1
Sparse Core Ops, SparseCore 0:
  23.0 35.8 all-gather.12
  60.4 33.0 all-gather.10
  95.8 126.4 all-gather.6
  250.4 52.5 reduce-scatter.2
  306.1 33.1 all-gather.8
  404.9 173.5 reduce-scatter.4
